TPU v7x, 32 devices: a whole 2x2x4 slice. The times are simulated.
32 devices in a mesh: facet: 4 (over z), sub: 2 (over y), wa: 4 (over x, core).
Axes of the slice: x: 2, y: 2, z: 4, core: 2. Of those that a mesh axis runs over, the one named last changes fastest.
Arguments:
- facet_data: bfloat16 [4, 128, 2, 8192], P('facet', ('sub', 'wa')), may hold values from -6 to 6
- window: float32 [8192], replicated, may hold values from 0.1 to 1
- screen_phase: float32 [1024, 1024], P('facet'), may hold values from -0.5 to 0.5
- facet_shift: int32 [4], replicated, may hold values from 0 to 1023
- sub_offset: int32 [8], replicated, may hold values from 0 to 8191
- win_start: int32 [4, 8], replicated, may hold values from 0 to 512
- win_extent: int32 [4, 8], replicated, may hold values from 256 to 512, as said below
- owner_slot: int32 [8], replicated, may hold values from 0 to 7, each once
- layer_w: int32 [8], replicated, may hold values from -12 to 12
Outputs:
- layers: bfloat16 [8, 8, 1024, 2, 1024], P('sub', 'wa', 'facet')
Inputs may be any that keep to these rules, and one draw needn't show every extreme that they name: win_start[f, j] + win_extent[f, j] <= 1024 for every facet f and subgrid j. A permutation of the subgrids; the subgrid with owner_slot = p belongs to sub index p // 4.
All inputs are finite; a program needn't handle non-finite values.
Results may differ from a plain program's by a relative error of at most 0.008.
Values may be sent and summed in bfloat16 or wider, within the bound.
A program may use at most 128 MiB of HBM per device.

v0:
```python
import functools
import math

import jax
import jax.numpy as jnp
import numpy as np
from jax import lax
from jax.experimental import pallas as pl
from jax.experimental.pallas import tpu as pltpu
from jax.sharding import PartitionSpec as P

RADIX = 4


def table(products, modulus, sign_value):
    angles = (sign_value * 2.0 * math.pi / modulus) * (products % modulus).astype(np.float64)
    return np.cos(angles), np.sin(angles)


def wave(products, modulus):
    angles = (2.0 * math.pi / modulus) * (products % modulus).astype(jnp.float32)
    return jnp.cos(angles), jnp.sin(angles)


def high(form, left, right):
    return jnp.einsum(form, left, right, precision=lax.Precision.HIGH)


def facet_spectrum(signal):
    strip_rows = signal.shape[0]
    facet_len = signal.shape[2]
    inner_len = 128
    outer_len = facet_len // inner_len
    grid_in = signal.reshape(strip_rows, 2 * outer_len, inner_len)
    outer_ids = np.arange(outer_len)
    inner_ids = np.arange(inner_len)
    c1, s1 = table(outer_ids[:, None] * outer_ids[None, :], outer_len, -1.0)
    first = np.block([[c1, -s1], [s1, c1]]).astype(np.float32)
    mid = high("zy,ryq->rzq", jnp.asarray(first), grid_in)
    mid_real = mid[:, :outer_len]
    mid_imag = mid[:, outer_len:]
    ct, st = table(outer_ids[:, None] * inner_ids[None, :], facet_len, -1.0)
    ct = jnp.asarray(ct.astype(np.float32))
    st = jnp.asarray(st.astype(np.float32))
    turned_real = mid_real * ct - mid_imag * st
    turned_imag = mid_real * st + mid_imag * ct
    turned = jnp.concatenate([turned_real, turned_imag], 2)
    c2, s2 = table(inner_ids[:, None] * inner_ids[None, :], inner_len, -1.0)
    scale = 1.0 / math.sqrt(facet_len)
    second = (np.block([[c2, s2], [-s2, c2]]) * scale).astype(np.float32)
    out = high("rpn,nq->rqp", turned, jnp.asarray(second))
    return out.reshape(strip_rows, 2, facet_len)


def finish_kernel(band, count, scale_rows, left_ref, right_ref, cos_ref, sin_ref, fwd_ref, out_ref, held):
    layer = pl.program_id(1)
    grid_size = cos_ref.shape[2]
    part = grid_size // RADIX

    @pl.when(layer == 0)
    def _():
        rows = jnp.dot(left_ref[...], right_ref[...], preferred_element_type=jnp.float32)
        held[...] = (rows * scale_rows).astype(jnp.bfloat16)

    real = held[:band, :].astype(jnp.float32)
    imag = held[band:, :].astype(jnp.float32)
    cos = cos_ref[0]
    sin = sin_ref[0]
    s_real = (real * cos - imag * sin).astype(jnp.bfloat16)
    s_imag = (real * sin + imag * cos).astype(jnp.bfloat16)
    pieces = []
    for p in range(RADIX):
        lo, hi = p * part, (p + 1) * part
        pair = jnp.concatenate([s_real[:, lo:hi], s_imag[:, lo:hi]], 1)
        got = jnp.dot(pair, fwd_ref[p], preferred_element_type=jnp.float32)
        pieces.append((got[:, :part], got[:, part:]))
    (ar, ai), (br, bi), (cr, ci), (dr, di) = pieces
    er, ei, fr, fi = ar + cr, ai + ci, ar - cr, ai - ci
    gr, gi, hr, hi_ = br + dr, bi + di, br - dr, bi - di
    reals = jnp.concatenate([er + gr, fr + hi_, er - gr, fr - hi_], 1)
    imags = jnp.concatenate([ei + gi, fi - hr, ei - gi, fi + hr], 1)
    out_ref[0, 0, :, 0, :] = reals.astype(jnp.bfloat16)
    out_ref[0, 0, :, 1, :] = imags.astype(jnp.bfloat16)


def finish(left, right, cos, sin, forward, slots, scale_rows):
    layers, band, grid_size = cos.shape
    count = right.shape[0]
    return pl.pallas_call(
        functools.partial(finish_kernel, band, count, scale_rows),
        grid=(slots, layers),
        out_shape=jax.ShapeDtypeStruct((slots, layers, band, 2, grid_size), jnp.bfloat16),
        in_specs=[
            pl.BlockSpec((2 * band, count), lambda s, l: (0, 0)),
            pl.BlockSpec((count, grid_size), lambda s, l: (0, s)),
            pl.BlockSpec((1, band, grid_size), lambda s, l: (l, 0, 0)),
            pl.BlockSpec((1, band, grid_size), lambda s, l: (l, 0, 0)),
            pl.BlockSpec(forward.shape, lambda s, l: (0, 0, 0)),
        ],
        out_specs=pl.BlockSpec((1, 1, band, 2, grid_size), lambda s, l: (s, l, 0, 0, 0)),
        scratch_shapes=[pltpu.VMEM((2 * band, grid_size), jnp.bfloat16)],
        compiler_params=pltpu.CompilerParams(vmem_limit_bytes=48 * 1024 * 1024),
        cost_estimate=pl.CostEstimate(flops=10_000_000_000, bytes_accessed=20_000_000, transcendentals=0),
    )(left, right, cos, sin, forward)


def local(
    facet_data,
    window,
    screen_phase,
    facet_shift,
    sub_offset,
    win_start,
    win_extent,
    owner_slot,
    layer_w,
):
    facets = lax.axis_size("facet")
    owners = lax.axis_size("sub")
    teams = lax.axis_size("wa")
    facet_id = lax.axis_index("facet")
    team_id = lax.axis_index("wa")
    strip_rows = facet_data.shape[1]
    facet_len = facet_data.shape[3]
    band = screen_phase.shape[0]
    grid_size = screen_phase.shape[1]
    width = grid_size // 2
    part = grid_size // RADIX
    total_subs = owner_slot.shape[0]
    slots = total_subs // owners
    share = strip_rows // facets
    strip_total = strip_rows * owners * teams

    spectrum = facet_spectrum(facet_data[0].astype(jnp.float32) * window)
    slot_ids = jnp.arange(total_subs, dtype=jnp.int32)
    chooser = (owner_slot[None, :] == slot_ids[:, None]).astype(jnp.int32)
    offset_slot = jnp.sum(chooser * sub_offset[None, :], axis=1)
    start_all = jnp.sum(win_start[:, None, :] * chooser[None], axis=2)
    extent_all = jnp.sum(win_extent[:, None, :] * chooser[None], axis=2)
    start_mine = lax.dynamic_index_in_dim(start_all, facet_id, 0, keepdims=False)
    extent_mine = lax.dynamic_index_in_dim(extent_all, facet_id, 0, keepdims=False)
    shift_value = lax.dynamic_index_in_dim(facet_shift, facet_id, 0, keepdims=False)
    begin = (offset_slot + start_mine) % facet_len
    steps = jnp.arange(width, dtype=jnp.int32)
    turn_cos, turn_sin = wave(shift_value * (start_mine[:, None] + steps[None, :]), grid_size)
    inside = steps[None, :] < extent_mine[:, None]
    turn_cos = jnp.where(inside, turn_cos, 0.0)
    turn_sin = jnp.where(inside, turn_sin, 0.0)
    wrapped = jnp.concatenate([spectrum, spectrum[:, :, :width]], 2)
    cuts = []
    for j in range(total_subs):
        picked = lax.dynamic_slice_in_dim(wrapped, begin[j], width, 2)
        cos_j = turn_cos[j][None, :]
        sin_j = turn_sin[j][None, :]
        cuts.append(
            jnp.concatenate(
                [
                    picked[:, 0] * cos_j - picked[:, 1] * sin_j,
                    picked[:, 0] * sin_j + picked[:, 1] * cos_j,
                ],
                1,
            ).astype(jnp.bfloat16)
        )
    sendable = jnp.stack(cuts).reshape(owners, slots, facets, share, 2 * width)
    sendable = sendable.transpose(2, 0, 1, 3, 4).reshape(facets * owners, slots * share, 2 * width)
    received = lax.all_to_all(sendable, ("facet", "sub"), split_axis=0, concat_axis=0, tiled=True)

    v_ids = np.arange(part)[None, :] * RADIX + np.arange(RADIX)[:, None]
    back_cos, back_sin = table(np.arange(width)[:, None] * v_ids.reshape(1, -1), grid_size, 1.0)
    back = np.block([[back_cos, back_sin], [-back_sin, back_cos]])
    moved = jnp.dot(
        received.reshape(facets * owners * slots * share, 2 * width),
        jnp.asarray(back.astype(jnp.bfloat16)),
        preferred_element_type=jnp.float32,
    ).reshape(facets, owners, slots, share, 2, grid_size)
    my_slot = lax.axis_index("sub") * slots
    start_slot = lax.dynamic_slice_in_dim(start_all, my_slot, slots, 1)
    ramp_cos, ramp_sin = wave(
        start_slot[:, :, None] * jnp.asarray(v_ids.reshape(1, 1, -1).astype(np.int32)), grid_size
    )
    scale_col = 1.0 / math.sqrt(facets * grid_size)
    ramp_cos = (ramp_cos * scale_col)[:, None, :, None, :]
    ramp_sin = (ramp_sin * scale_col)[:, None, :, None, :]
    col_real = jnp.sum(moved[:, :, :, :, 0] * ramp_cos - moved[:, :, :, :, 1] * ramp_sin, 0)
    col_imag = jnp.sum(moved[:, :, :, :, 0] * ramp_sin + moved[:, :, :, :, 1] * ramp_cos, 0)
    image = jnp.stack([col_real, col_imag], 0).astype(jnp.bfloat16)
    image = image.transpose(0, 1, 3, 2, 4).reshape(2 * owners * share, slots * grid_size)
    right = lax.all_gather(image, ("facet", "wa"), axis=0, tiled=True)

    f_ids, t_ids, c_ids, o_ids, r_ids = np.meshgrid(
        np.arange(facets), np.arange(teams), np.arange(2), np.arange(owners), np.arange(share), indexing="ij"
    )
    global_row = ((o_ids * teams + t_ids) * strip_rows + f_ids * share + r_ids).reshape(-1)
    is_imag = c_ids.reshape(-1)
    all_cos, all_sin = table(np.arange(grid_size)[:, None] * global_row[None, :], grid_size, -1.0)
    real_rows = np.where(is_imag == 1, -all_sin, all_cos).reshape(facets, band, -1)
    imag_rows = np.where(is_imag == 1, all_cos, all_sin).reshape(facets, band, -1)
    left_all = np.concatenate([real_rows, imag_rows], 1).astype(jnp.bfloat16)
    left = lax.dynamic_index_in_dim(jnp.asarray(left_all), facet_id, 0, keepdims=False)

    layer_dev = layer_w.shape[0] // teams
    levels = lax.dynamic_slice_in_dim(layer_w, team_id * layer_dev, layer_dev, 0)
    pick = np.zeros((grid_size, grid_size), np.float32)
    pick[v_ids.reshape(-1), np.arange(grid_size)] = 1.0
    ordered = jnp.dot(
        screen_phase,
        jnp.asarray(pick.astype(jnp.bfloat16)).astype(jnp.float32),
        precision=lax.Precision.HIGHEST,
    )
    angles = levels.astype(jnp.float32)[:, None, None] * ordered[None]
    cos = jnp.cos(angles)
    sin = jnp.sin(angles)

    fwd_cos, fwd_sin = table(v_ids[:, :, None] * np.arange(part)[None, None, :], grid_size, -1.0)
    rounded = lambda x: x.astype(jnp.bfloat16).astype(np.float64)
    fwd_cos, fwd_sin = rounded(fwd_cos), rounded(fwd_sin)
    forward = np.concatenate(
        [np.concatenate([fwd_cos, fwd_sin], 2), np.concatenate([-fwd_sin, fwd_cos], 2)], 1
    )
    forward = (forward / math.sqrt(grid_size)).astype(jnp.bfloat16)
    return finish(left, right, cos, sin, jnp.asarray(forward), slots, 1.0 / math.sqrt(strip_total))


def solution(mesh):
    in_specs = (
        P("facet", ("sub", "wa"), None, None),
        P(),
        P("facet", None),
        P(),
        P(),
        P(),
        P(),
        P(),
        P(),
    )
    out_specs = P("sub", "wa", "facet", None, None)
    return jax.shard_map(local, mesh=mesh, in_specs=in_specs, out_specs=out_specs, check_vma=False)
```

profile of v0, /device:TPU:0, one launch (start us, length us, event | category | flops | bytes accessed | tf_op | source)
XLA Modules:
  0.0 127.1 jit_solution(14068415405786298980)
XLA Ops:
  6.5 0.7 fusion.41
  7.3 0.8 select_reduce_fusion
  8.1 0.9 multiply_reduce_fusion
  19.7 1.3 %dynamic_slice.49 = s32[1]{0:T(128)} dynamic-slice(s32[4]{0:T(128)} %param.21, s32[]{:T(128)S(6)} %select_n.72), dynamic_slice_sizes={1} | dynamic-slice | bytes 12 | tf_op jit(solution)/shard_map/jit(dynamic_index_in_dim)/dynamic_slice | solution.py:142
  21.0 1.4 %reshape.1385 = f32[16,128,128]{2,1,0:T(8,128)S(1)} reshape(bf16[1,16,2,8192]{3,2,1,0:T(2,128)(2,1)} %param.18) | data formatting | bytes 1572864 | tf_op jit(solution)/shard_map/convert_element_type | solution.py:134
  22.4 0.8 mul.600
  23.2 1.5 %convolution_bitcast_fusion.2 = f32[16,128,128]{2,1,0:T(8,128)S(1)} fusion(f32[128,128,1]{1,0,2:T(8,128)} %constant.111, f32[16,128,128]{2,1,0:T(8,128)S(1)} %reshape.1385, f32[128,128]{1,0:T(8,128)S(1)} %bitcast.279), kind=kOutput, calls=%fused_computation.12 | convolution fusion | flops 201588736 | bytes 2228224 | tf_op jit(solution)/shard_map/zy,ryq->rzq/dot_general | solution.py:26
  24.9 1.6 %convolution_bitcast_fusion.1 = f32[16,256,64]{1,2,0:T(8,128)} fusion(f32[256,256,1]{1,0,2:T(8,128)S(1)} %copy-done.2, f32[16,64,128]{2,1,0:T(8,128)S(1)} %get-tuple-element.20, f32[16,64,128]{2,1,0:T(8,128)S(1)} %get-tuple-element.19), kind=kOutput, calls=%fused_computation.11 | convolution fusion | flops 402915328 | bytes 2359296 | tf_op jit(solution)/shard_map/rpn,nq->rqp/dot_general | solution.py:26
  26.4 1.8 %copy.65 = f32[16,256,64]{2,1,0:T(8,128)S(1)} copy(f32[16,256,64]{1,2,0:T(8,128)} %convolution_bitcast_fusion.1) | data formatting | bytes 2097152 | tf_op jit(solution)/shard_map/rpn,nq->rqp/transpose | solution.py:26
  28.3 2.0 %reshape.1381 = f32[16,2,8192]{2,1,0:T(2,128)} reshape(f32[16,256,64]{2,1,0:T(8,128)S(1)} %copy.65) | data formatting | bytes 2097152 | tf_op jit(solution)/shard_map/reshape | solution.py:52
  30.3 0.8 slice.248
  36.1 0.8 cosine_select_fusion
  37.0 2.5 %fusion.7 = (f32[16,2,512]{2,1,0:T(2,128)S(1)}, f32[16,2,512]{2,1,0:T(2,128)S(1)}, f32[16,2,512]{2,1,0:T(2,128)S(1)}, f32[16,2,512]{2,1,0:T(2,128)S(1)}, f32[16,...) fusion(s32[]{:T(128)S(6)} %select_n.84, ...), kind=kLoop, calls=%fused_computation.33 | loop fusion | flops 131072 | bytes 1638432 | tf_op jit(solution)/shard_map/concatenate | solution.py:149
  40.5 0.8 reshape.1383
  41.2 7.3 %all-to-all-start = ((bf16[8,16,1024]{2,1,0:T(8,128)(2,1)}), bf16[8,16,1024]{2,1,0:T(8,128)(2,1)S(1)}, u32[]{:S(2)}, u32[]{:S(2)}) async-start(bf16[8,16,1024]{2,1,0:T(8,128)(2,1)} %reshape.1383), calls=%async_computation | async-start | bytes 524288 | tf_op jit(solution)/shard_map/all_to_all | solution.py:166
  49.4 8.0 %all-to-all-done = bf16[8,16,1024]{2,1,0:T(8,128)(2,1)S(1)} async-done(((bf16[8,16,1024]{2,1,0:T(8,128)(2,1)}), bf16[8,16,1024]{2,1,0:T(8,128)(2,1)S(1)}, u32[]{:S(2)}, u32[]{:S(2)}) %all-to-all-start) | async-done | bytes 262176 | tf_op jit(solution)/shard_map/all_to_all | solution.py:166
  57.5 3.9 %fusion.5 = f32[4,2,4,4,2,1024]{5,3,4,2,1,0:T(4,128)S(1)} fusion(bf16[2,1024,1024,1,1,1]{2,1,0,5,4,3:T(8,128)(2,1)} %constant.113, bf16[4,2,4,4,1024,1]{4,3,2,1,0,5:T(4,128)(2,1)S(1)} %reshape.1388), kind=kOutput, calls=%fused_computation.25 | convolution fusion | flops 536870912 | bytes 5505024 | tf_op jit(solution)/shard_map/dot_general | solution.py:171
  62.8 4.0 %convolution_bitcast_fusion = f32[256,1024]{0,1:T(8,128)S(1)} fusion(bf16[1024,1024]{1,0:T(8,128)(2,1)} %constant.105.clone, f32[256,1024]{1,0:T(8,128)S(1)} %copy-done), kind=kOutput, calls=%fused_computation.10 | convolution fusion | flops 3221225472 | bytes 4194304 | tf_op jit(solution)/shard_map/dot_general | solution.py:205
  66.8 1.3 %copy.77 = f32[256,1024]{1,0:T(8,128)} copy(f32[256,1024]{0,1:T(8,128)S(1)} %convolution_bitcast_fusion) | data formatting | bytes 2097152 | tf_op jit(solution)/shard_map/dot_general | solution.py:205
  68.2 1.0 dynamic-slice_bitcast_fusion.left_ref
  69.1 9.6 %multiply_sine_fusion = (f32[2,256,1024]{2,1,0:T(8,128)}, f32[2,256,1024]{2,1,0:T(8,128)S(1)}) fusion(f32[256,1024]{1,0:T(8,128)} %copy.77, f32[2]{0:T(128)S(1)} %dynamic-slice_convert_fusion), kind=kLoop, calls=%fused_computation | loop fusion | flops 524288 | bytes 5242888 | tf_op jit(solution)/shard_map/sin | solution.py:212
  78.8 24.6 %all-gather.2.cloned.1.call-done.right_ref = bf16[256,4096]{1,0:T(8,128)(2,1)} async-done(((bf16[16,4096]{1,0:T(8,128)(2,1)}), bf16[256,4096]{1,0:T(8,128)(2,1)}) %all-gather.2.cloned.1.call-update) | async-done | bytes 2097168 | tf_op jit(solution)/shard_map/all_gather | solution.py:188
  103.4 1.6 %copy-done.1 = bf16[256,4096]{1,0:T(8,128)(2,1)S(1)} copy-done((bf16[256,4096]{1,0:T(8,128)(2,1)S(1)}, bf16[256,4096]{1,0:T(8,128)(2,1)}, u32[]{:S(2)}) %copy-start.1) | copy-done | bytes 2097176
  105.0 15.3 %shard_map.172 = bf16[4,2,256,2,1024]{4,3,2,1,0:T(2,128)(2,1)} custom-call(bf16[512,256]{1,0:T(8,128)(2,1)S(1)} %dynamic-slice_bitcast_fusion.left_ref, bf16[256,4096]{1,0:T(8,128)(2,1)S(1)} %copy-done.1, f32[2,256,1024]{2,1,0:T(8,128)S(1)} %get-tuple-element.22.cos_ref, f32[2,256,1024]{2,1,0:T(8,128)} %get-tuple-element.21.sin_ref, ...), custom_call_target="tpu_custom_call" | custom-call | flops 10000000000 | bytes 20000000 | tf_op jit(solution)/shard_map/pallas_call | solution.py:89
  (50 shorter events, 4.1 us)
Async XLA Ops:
  6.5 56.2 %copy-start = (f32[256,1024]{1,0:T(8,128)S(1)}, f32[256,1024]{1,0:T(8,128)}, u32[]{:S(2)}) copy-start(f32[256,1024]{1,0:T(8,128)} %param.20) | copy-start | bytes 3145732
  6.5 18.1 %copy-start.3 = (f32[64,128]{1,0:T(8,128)S(1)}, f32[64,128]{1,0:T(8,128)}, u32[]{:S(2)}) copy-start(f32[64,128]{1,0:T(8,128)} %constant.100.clone) | copy-start | bytes 98308
  6.5 18.1 %copy-start.4 = (f32[64,128]{1,0:T(8,128)S(1)}, f32[64,128]{1,0:T(8,128)}, u32[]{:S(2)}) copy-start(f32[64,128]{1,0:T(8,128)} %constant.99.clone) | copy-start | bytes 98308
  23.2 1.7 %copy-start.2 = (f32[256,256,1]{1,0,2:T(8,128)S(1)}, f32[256,256,1]{1,0,2:T(8,128)}, u32[]{:S(2)}) copy-start(f32[256,256,1]{1,0,2:T(8,128)} %constant.112) | copy-start | bytes 786436
  39.7 9.1 %copy-start.5 = (s32[1024]{0:T(1024)S(1)}, s32[1024]{0:T(1024)}, u32[]{:S(2)}) copy-start(s32[1024]{0:T(1024)} %constant.110) | copy-start | bytes 12292
  41.2 16.2 %all-to-all-start = ((bf16[8,16,1024]{2,1,0:T(8,128)(2,1)}), bf16[8,16,1024]{2,1,0:T(8,128)(2,1)S(1)}, u32[]{:S(2)}, u32[]{:S(2)}) async-start(bf16[8,16,1024]{2,1,0:T(8,128)(2,1)} %reshape.1383), calls=%async_computation | async-start | bytes 524288 | tf_op jit(solution)/shard_map/all_to_all | solution.py:166
  48.5 54.9 %all-gather.2.cloned.1.call-start = ((), (), s32[]{:S(2)}) async-start(), calls=%async_computation.1 | async-start | bytes 2228224 | tf_op jit(solution)/shard_map/all_gather | solution.py:188
  66.8 1.3 %copy-start.6 = (s32[8]{0:T(128)S(1)}, s32[8]{0:T(128)}, u32[]{:S(2)}) copy-start(s32[8]{0:T(128)} %param.26) | copy-start | bytes 100
  103.4 1.6 %copy-start.1 = (bf16[256,4096]{1,0:T(8,128)(2,1)S(1)}, bf16[256,4096]{1,0:T(8,128)(2,1)}, u32[]{:S(2)}) copy-start(bf16[256,4096]{1,0:T(8,128)(2,1)} %all-gather.2.cloned.1.call-done.right_ref) | copy-start | bytes 6291460
Sparse Core Ops, SparseCore 0:
  62.9 40.4 all-gather.1
where the time goes:
time: 128 us; the launch traced here: 127 us
  waiting for transfers between devices  32.7 us (26%)
  between operations  28.8 us (22%)
  other arithmetic  17 us (13%)
  Pallas kernels  15.3 us (12%)
  local copies, waits for them, and re-layouts  15.1 us (12%)
  matrix products  10.8 us (8%)
  starting transfers between devices  7.48 us (6%)
    all_gather x1, waiting for transfers between devices, local(): right = lax.all_gather(image, ('facet', 'wa'), axis=0, tiled=True)  24.6 us
    pallas_call x1, Pallas kernels, finish(): pl.pallas_call(functools.partial(finish_kernel, band, count, scale_rows),...  15.3 us
    sin x1, other arithmetic, local(): sin = jnp.sin(angles)  9.62 us
    all_to_all x1, waiting for transfers between devices, local(): lax.all_to_all(sendable, ('facet', 'sub'), split_axis=0, concat_axis=0, t...  8.01 us
    all_to_all x1, starting transfers between devices, local(): lax.all_to_all(sendable, ('facet', 'sub'), split_axis=0, concat_axis=0, t...  7.27 us
    dot_general x1, matrix products, local(): jnp.dot(screen_phase, jnp.asarray(pick.astype(jnp.bfloat16)).astype(jnp.f...  3.97 us
    dot_general x1, matrix products, local(): jnp.dot(received.reshape(facets * owners * slots * share, 2 * width), jnp...  3.86 us
    dot_general x2, matrix products, high(): return jnp.einsum(form, left, right, precision=lax.Precision.HIGH)  3.02 us
  transfers between devices with their start and end apart: 2, of which 2 were waited for; matrix products, arithmetic and copies ran while one was open for 13% of the time, Pallas kernels for 0%

commit v1 on v0

--- a/solution.py
+++ b/solution.py
@@ -102,6 +102,15 @@
         compiler_params=pltpu.CompilerParams(vmem_limit_bytes=48 * 1024 * 1024),
         cost_estimate=pl.CostEstimate(flops=10_000_000_000, bytes_accessed=20_000_000, transcendentals=0),
     )(left, right, cos, sin, forward)
+
+
+def doubled(block, axis, size, steps):
+    order = [0]
+    for step in steps:
+        other = lax.ppermute(block, axis, [(i, i ^ step) for i in range(size)])
+        block = jnp.concatenate([block, other], 0)
+        order = order + [o ^ step for o in order]
+    return block, order
 
 
 def local(
@@ -185,18 +194,25 @@
     col_imag = jnp.sum(moved[:, :, :, :, 0] * ramp_sin + moved[:, :, :, :, 1] * ramp_cos, 0)
     image = jnp.stack([col_real, col_imag], 0).astype(jnp.bfloat16)
     image = image.transpose(0, 1, 3, 2, 4).reshape(2 * owners * share, slots * grid_size)
-    right = lax.all_gather(image, ("facet", "wa"), axis=0, tiled=True)
-
-    f_ids, t_ids, c_ids, o_ids, r_ids = np.meshgrid(
-        np.arange(facets), np.arange(teams), np.arange(2), np.arange(owners), np.arange(share), indexing="ij"
-    )
-    global_row = ((o_ids * teams + t_ids) * strip_rows + f_ids * share + r_ids).reshape(-1)
-    is_imag = c_ids.reshape(-1)
-    all_cos, all_sin = table(np.arange(grid_size)[:, None] * global_row[None, :], grid_size, -1.0)
-    real_rows = np.where(is_imag == 1, -all_sin, all_cos).reshape(facets, band, -1)
-    imag_rows = np.where(is_imag == 1, all_cos, all_sin).reshape(facets, band, -1)
-    left_all = np.concatenate([real_rows, imag_rows], 1).astype(jnp.bfloat16)
-    left = lax.dynamic_index_in_dim(jnp.asarray(left_all), facet_id, 0, keepdims=False)
+    facet_steps = [1 << i for i in range(facets.bit_length() - 1)]
+    team_steps = [1 << i for i in range(teams.bit_length() - 1)][::-1]
+    right, facet_order = doubled(image, "facet", facets, facet_steps)
+    right, team_order = doubled(right, "wa", teams, team_steps)
+
+    me_f, me_t, t_ids, f_ids, c_ids, o_ids, r_ids = np.meshgrid(
+        np.arange(facets), np.arange(teams), np.array(team_order), np.array(facet_order),
+        np.arange(2), np.arange(owners), np.arange(share), indexing="ij"
+    )
+    global_row = (o_ids * teams + (t_ids ^ me_t)) * strip_rows + (f_ids ^ me_f) * share + r_ids
+    global_row = global_row.reshape(facets, teams, 1, -1)
+    is_imag = c_ids.reshape(facets, teams, 1, -1)
+    my_rows = np.arange(grid_size).reshape(facets, 1, band, 1)
+    all_cos, all_sin = table(my_rows * global_row, grid_size, -1.0)
+    real_rows = np.where(is_imag == 1, -all_sin, all_cos)
+    imag_rows = np.where(is_imag == 1, all_cos, all_sin)
+    left_all = np.concatenate([real_rows, imag_rows], 2).astype(jnp.bfloat16)
+    left_all = left_all.reshape(facets * teams, 2 * band, -1)
+    left = lax.dynamic_index_in_dim(jnp.asarray(left_all), facet_id * teams + team_id, 0, keepdims=False)
 
     layer_dev = layer_w.shape[0] // teams
     levels = lax.dynamic_slice_in_dim(layer_w, team_id * layer_dev, layer_dev, 0)

time: 128 us -> 105 us (0.82)
  between operations: 28.8 us -> 15.4 us
  waiting for transfers between devices: 32.7 us -> 24.1 us
  starting transfers between devices: 7.48 us -> 11.2 us
  local copies, waits for them, and re-layouts: 15.1 us -> 12.3 us
  matrix products: 10.8 us -> 9.35 us
    all_gather x1 -> x0, waiting for transfers between devices: 24.6 us -> none  [local(): right = lax.all_gather(image, ('facet', 'wa'), axis=0, tiled=True)]
    ppermute x0 -> x4, waiting for transfers between devices: none -> 15.8 us  [doubled(): other = lax.ppermute(block, axis, [(i, i ^ step) for i in range(size)])]
    ppermute x0 -> x4, starting transfers between devices: none -> 3.88 us  [doubled(): other = lax.ppermute(block, axis, [(i, i ^ step) for i in range(size)])]
    unnamed x15 -> x19, local copies, waits for them, and re-layouts: 2.32 us -> 0.45 us
    dot_general x1, matrix products: 3.97 us -> 2.46 us  [local(): jnp.dot(screen_phase, jnp.asarray(pick.astype(jnp.bfloat16)).astype(jnp.f...]
  transfers between devices with their start and end apart: 2 -> 5, of which waited for: 2 -> 5; matrix products, arithmetic and copies ran while one was open for 13% -> 13% of each run, Pallas kernels for 0% -> 0%
where the time goes in v1:
time: 105 us; the launch traced here: 104 us
  waiting for transfers between devices  24.1 us (23%)
  other arithmetic  16.1 us (15%)
  between operations  15.4 us (15%)
  Pallas kernels  15.3 us (15%)
  local copies, waits for them, and re-layouts  12.3 us (12%)
  starting transfers between devices  11.2 us (11%)
  matrix products  9.35 us (9%)
    ppermute x4, waiting for transfers between devices, doubled(): other = lax.ppermute(block, axis, [(i, i ^ step) for i in range(size)])  15.8 us
    pallas_call x1, Pallas kernels, finish(): pl.pallas_call(functools.partial(finish_kernel, band, count, scale_rows),...  15.3 us
    sin x1, other arithmetic, local(): sin = jnp.sin(angles)  8.62 us
    all_to_all x1, waiting for transfers between devices, local(): lax.all_to_all(sendable, ('facet', 'sub'), split_axis=0, concat_axis=0, t...  8.24 us
    all_to_all x1, starting transfers between devices, local(): lax.all_to_all(sendable, ('facet', 'sub'), split_axis=0, concat_axis=0, t...  7.32 us
    ppermute x4, starting transfers between devices, doubled(): other = lax.ppermute(block, axis, [(i, i ^ step) for i in range(size)])  3.88 us
    dot_general x1, matrix products, local(): jnp.dot(received.reshape(facets * owners * slots * share, 2 * width), jnp...  3.87 us
    dot_general x2, matrix products, high(): return jnp.einsum(form, left, right, precision=lax.Precision.HIGH)  3.02 us
  transfers between devices with their start and end apart: 5, of which 5 were waited for; matrix products, arithmetic and copies ran while one was open for 13% of the time, Pallas kernels for 0%

profile of v1, /device:TPU:0, one launch (start us, length us, event | category | flops | bytes accessed | tf_op | source)
XLA Modules:
  0.0 103.8 jit_solution(16551782262880271299)
XLA Ops:
  0.8 0.8 select_reduce_fusion
  1.5 0.9 multiply_reduce_fusion
  13.1 1.3 %dynamic_slice.49 = s32[1]{0:T(128)} dynamic-slice(s32[4]{0:T(128)} %param.21, s32[]{:T(128)S(6)} %select_n.75), dynamic_slice_sizes={1} | dynamic-slice | bytes 12 | tf_op jit(solution)/shard_map/jit(dynamic_index_in_dim)/dynamic_slice | solution.py:151
  14.5 1.4 %reshape.1385 = f32[16,128,128]{2,1,0:T(8,128)S(1)} reshape(bf16[1,16,2,8192]{3,2,1,0:T(2,128)(2,1)} %param.18) | data formatting | bytes 1572864 | tf_op jit(solution)/shard_map/convert_element_type | solution.py:143
  16.6 1.5 %convolution_bitcast_fusion.2 = f32[16,128,128]{2,1,0:T(8,128)S(1)} fusion(f32[128,128,1]{1,0,2:T(8,128)} %constant.112, f32[16,128,128]{2,1,0:T(8,128)S(1)} %reshape.1385, f32[128,128]{1,0:T(8,128)S(1)} %bitcast.283), kind=kOutput, calls=%fused_computation.12 | convolution fusion | flops 201588736 | bytes 2228224 | tf_op jit(solution)/shard_map/zy,ryq->rzq/dot_general | solution.py:26
  18.3 1.6 %convolution_bitcast_fusion.1 = f32[16,256,64]{1,2,0:T(8,128)} fusion(f32[256,256,1]{1,0,2:T(8,128)S(1)} %copy-done.2, f32[16,64,128]{2,1,0:T(8,128)S(1)} %get-tuple-element.20, f32[16,64,128]{2,1,0:T(8,128)S(1)} %get-tuple-element.19), kind=kOutput, calls=%fused_computation.11 | convolution fusion | flops 402915328 | bytes 2359296 | tf_op jit(solution)/shard_map/rpn,nq->rqp/dot_general | solution.py:26
  19.9 1.8 %copy.65 = f32[16,256,64]{2,1,0:T(8,128)S(1)} copy(f32[16,256,64]{1,2,0:T(8,128)} %convolution_bitcast_fusion.1) | data formatting | bytes 2097152 | tf_op jit(solution)/shard_map/rpn,nq->rqp/transpose | solution.py:26
  21.7 2.0 %reshape.1381 = f32[16,2,8192]{2,1,0:T(2,128)} reshape(f32[16,256,64]{2,1,0:T(8,128)S(1)} %copy.65) | data formatting | bytes 2097152 | tf_op jit(solution)/shard_map/reshape | solution.py:52
  23.7 0.8 slice.248
  29.6 0.8 cosine_select_fusion
  30.4 2.5 %fusion.7 = (f32[16,2,512]{2,1,0:T(2,128)S(1)}, f32[16,2,512]{2,1,0:T(2,128)S(1)}, f32[16,2,512]{2,1,0:T(2,128)S(1)}, f32[16,2,512]{2,1,0:T(2,128)S(1)}, f32[16,...) fusion(s32[]{:T(128)S(6)} %select_n.87, ...), kind=kLoop, calls=%fused_computation.36 | loop fusion | flops 131072 | bytes 1638432 | tf_op jit(solution)/shard_map/concatenate | solution.py:158
  34.6 7.3 %all-to-all-start = ((bf16[8,16,1024]{2,1,0:T(8,128)(2,1)}), bf16[8,16,1024]{2,1,0:T(8,128)(2,1)S(1)}, u32[]{:S(2)}, u32[]{:S(2)}) async-start(bf16[8,16,1024]{2,1,0:T(8,128)(2,1)} %reshape.1383), calls=%async_computation | async-start | bytes 524288 | tf_op jit(solution)/shard_map/all_to_all | solution.py:175
  42.7 8.2 %all-to-all-done = bf16[8,16,1024]{2,1,0:T(8,128)(2,1)S(1)} async-done(((bf16[8,16,1024]{2,1,0:T(8,128)(2,1)}), bf16[8,16,1024]{2,1,0:T(8,128)(2,1)S(1)}, u32[]{:S(2)}, u32[]{:S(2)}) %all-to-all-start) | async-done | bytes 262176 | tf_op jit(solution)/shard_map/all_to_all | solution.py:175
  51.0 3.9 %fusion.5 = f32[4,2,4,4,2,1024]{5,3,4,2,1,0:T(4,128)S(1)} fusion(bf16[2,1024,1024,1,1,1]{2,1,0,5,4,3:T(8,128)(2,1)} %constant.114, bf16[4,2,4,4,1024,1]{4,3,2,1,0,5:T(4,128)(2,1)S(1)} %reshape.1388), kind=kOutput, calls=%fused_computation.28 | convolution fusion | flops 536870912 | bytes 5505024 | tf_op jit(solution)/shard_map/dot_general | solution.py:180
  55.6 1.1 %collective-permute-start = (bf16[16,4096]{1,0:T(8,128)(2,1)S(1)}, bf16[16,4096]{1,0:T(8,128)(2,1)S(1)}, u32[]{:S(2)}, u32[]{:S(2)}) collective-permute-start(bf16[16,4096]{1,0:T(8,128)(2,1)S(1)} %bitcast.276), channel_id=1, source_target_pairs={{0,8},{8,0},{16,24},{24,16},{1,9},{9,1},{17,25},{25,17},{2,10},{10... | collective-permute-start | bytes 393224 | tf_op jit(solution)/shard_map/ppermute | solution.py:110
  56.7 2.5 %convolution_bitcast_fusion = f32[256,1024]{0,1:T(8,128)S(1)} fusion(bf16[1024,1024]{1,0:T(8,128)(2,1)S(1)} %copy-done.1, f32[256,1024]{1,0:T(8,128)S(1)} %copy-done), kind=kOutput, calls=%fused_computation.10 | convolution fusion | flops 3221225472 | bytes 4194304 | tf_op jit(solution)/shard_map/dot_general | solution.py:221
  60.6 1.1 %collective-permute-start.1 = (bf16[32,4096]{1,0:T(8,128)(2,1)S(1)}, bf16[32,4096]{1,0:T(8,128)(2,1)S(1)}, u32[]{:S(2)}, u32[]{:S(2)}) collective-permute-start(bf16[32,4096]{1,0:T(8,128)(2,1)S(1)} %pad_maximum_fusion.2), channel_id=1, source_target_pairs={{0,16},{8,24},{16,0},{24,8},{1,17},{9,25},{17,1},{25,9},{2,18},{10... | collective-permute-start | bytes 786440 | tf_op jit(solution)/shard_map/ppermute | solution.py:110
  61.8 8.6 %multiply_sine_fusion = (f32[2,256,1024]{2,1,0:T(8,128)}, f32[2,256,1024]{2,1,0:T(8,128)S(1)}) fusion(f32[256,1024]{1,0:T(8,128)S(1)} %copy.77, f32[2]{0:T(128)S(1)} %dynamic-slice_convert_fusion), kind=kLoop, calls=%fused_computation | loop fusion | flops 524288 | bytes 5242888 | tf_op jit(solution)/shard_map/sin | solution.py:228
  70.4 2.2 %collective-permute-done.1 = bf16[32,4096]{1,0:T(8,128)(2,1)S(1)} collective-permute-done((bf16[32,4096]{1,0:T(8,128)(2,1)S(1)}, bf16[32,4096]{1,0:T(8,128)(2,1)S(1)}, u32[]{:S(2)}, u32[]{:S(2)}) %collective-permute-start.1) | collective-permute-done | bytes 262176 | tf_op jit(solution)/shard_map/ppermute | solution.py:110
  72.6 1.6 %collective-permute-start.2 = (bf16[64,4096]{1,0:T(8,128)(2,1)S(1)}, bf16[64,4096]{1,0:T(8,128)(2,1)S(1)}, u32[]{:S(2)}, u32[]{:S(2)}) collective-permute-start(bf16[64,4096]{1,0:T(8,128)(2,1)S(1)} %pad_maximum_fusion.1), channel_id=1, source_target_pairs={{0,2},{1,3},{2,0},{3,1},{4,6},{5,7},{6,4},{7,5},{8,10},{9,11},{10,... | collective-permute-start | bytes 1572872 | tf_op jit(solution)/shard_map/ppermute | solution.py:110
  74.1 1.0 dynamic-slice_bitcast_fusion.left_ref
  75.1 10.4 %collective-permute-done.2 = bf16[64,4096]{1,0:T(8,128)(2,1)S(1)} collective-permute-done((bf16[64,4096]{1,0:T(8,128)(2,1)S(1)}, bf16[64,4096]{1,0:T(8,128)(2,1)S(1)}, u32[]{:S(2)}, u32[]{:S(2)}) %collective-permute-start.2) | collective-permute-done | bytes 524320 | tf_op jit(solution)/shard_map/ppermute | solution.py:110
  85.8 2.6 %collective-permute-done.3 = bf16[128,4096]{1,0:T(8,128)(2,1)S(1)} collective-permute-done((bf16[128,4096]{1,0:T(8,128)(2,1)S(1)}, bf16[128,4096]{1,0:T(8,128)(2,1)S(1)}, u32[]{:S(2)}, u32[]{:S(2)}) %collective-permute-start.3) | collective-permute-done | bytes 1048608 | tf_op jit(solution)/shard_map/ppermute | solution.py:110
  88.5 15.3 %shard_map.172 = bf16[4,2,256,2,1024]{4,3,2,1,0:T(2,128)(2,1)} custom-call(bf16[512,256]{1,0:T(8,128)(2,1)S(1)} %dynamic-slice_bitcast_fusion.left_ref, bf16[256,4096]{1,0:T(8,128)(2,1)S(1)} %constant_dynamic-update-slice_fusion.right_ref, f32[2,256,1024]{2,1,0:T(8,128)S(1)} %get-tuple-element.22.cos_ref, f32[2,256,1024]{2,1,0:T(8,128)} %get-tuple-element.21.sin_ref, ...), custom_call_target="tpu_custom_call" | custom-call | flops 10000000000 | bytes 20000000 | tf_op jit(solution)/shard_map/pallas_call | solution.py:89
  (63 shorter events, 7.2 us)
Async XLA Ops:
  0.0 56.7 %copy-start = (f32[256,1024]{1,0:T(8,128)S(1)}, f32[256,1024]{1,0:T(8,128)}, u32[]{:S(2)}) copy-start(f32[256,1024]{1,0:T(8,128)} %param.20) | copy-start | bytes 3145732
  0.0 18.1 %copy-start.3 = (f32[64,128]{1,0:T(8,128)S(1)}, f32[64,128]{1,0:T(8,128)}, u32[]{:S(2)}) copy-start(f32[64,128]{1,0:T(8,128)} %constant.101.clone) | copy-start | bytes 98308
  0.0 18.1 %copy-start.4 = (f32[64,128]{1,0:T(8,128)S(1)}, f32[64,128]{1,0:T(8,128)}, u32[]{:S(2)}) copy-start(f32[64,128]{1,0:T(8,128)} %constant.100.clone) | copy-start | bytes 98308
  16.6 1.7 %copy-start.2 = (f32[256,256,1]{1,0,2:T(8,128)S(1)}, f32[256,256,1]{1,0,2:T(8,128)}, u32[]{:S(2)}) copy-start(f32[256,256,1]{1,0,2:T(8,128)} %constant.113) | copy-start | bytes 786436
  33.1 8.9 %copy-start.5 = (s32[1024]{0:T(1024)S(1)}, s32[1024]{0:T(1024)}, u32[]{:S(2)}) copy-start(s32[1024]{0:T(1024)} %constant.111) | copy-start | bytes 12292
  34.6 16.2 %all-to-all-start = ((bf16[8,16,1024]{2,1,0:T(8,128)(2,1)}), bf16[8,16,1024]{2,1,0:T(8,128)(2,1)S(1)}, u32[]{:S(2)}, u32[]{:S(2)}) async-start(bf16[8,16,1024]{2,1,0:T(8,128)(2,1)} %reshape.1383), calls=%async_computation | async-start | bytes 524288 | tf_op jit(solution)/shard_map/all_to_all | solution.py:175
  54.9 1.8 %copy-start.1 = (bf16[1024,1024]{1,0:T(8,128)(2,1)S(1)}, bf16[1024,1024]{1,0:T(8,128)(2,1)}, u32[]{:S(2)}) copy-start(bf16[1024,1024]{1,0:T(8,128)(2,1)} %constant.106.clone) | copy-start | bytes 6291460
  55.6 5.0 %collective-permute-start = (bf16[16,4096]{1,0:T(8,128)(2,1)S(1)}, bf16[16,4096]{1,0:T(8,128)(2,1)S(1)}, u32[]{:S(2)}, u32[]{:S(2)}) collective-permute-start(bf16[16,4096]{1,0:T(8,128)(2,1)S(1)} %bitcast.276), channel_id=1, source_target_pairs={{0,8},{8,0},{16,24},{24,16},{1,9},{9,1},{17,25},{25,17},{2,10},{10... | collective-permute-start | bytes 393224 | tf_op jit(solution)/shard_map/ppermute | solution.py:110
  59.2 0.7 copy-start.6
  60.6 11.9 %collective-permute-start.1 = (bf16[32,4096]{1,0:T(8,128)(2,1)S(1)}, bf16[32,4096]{1,0:T(8,128)(2,1)S(1)}, u32[]{:S(2)}, u32[]{:S(2)}) collective-permute-start(bf16[32,4096]{1,0:T(8,128)(2,1)S(1)} %pad_maximum_fusion.2), channel_id=1, source_target_pairs={{0,16},{8,24},{16,0},{24,8},{1,17},{9,25},{17,1},{25,9},{2,18},{10... | collective-permute-start | bytes 786440 | tf_op jit(solution)/shard_map/ppermute | solution.py:110
  72.6 13.0 %collective-permute-start.2 = (bf16[64,4096]{1,0:T(8,128)(2,1)S(1)}, bf16[64,4096]{1,0:T(8,128)(2,1)S(1)}, u32[]{:S(2)}, u32[]{:S(2)}) collective-permute-start(bf16[64,4096]{1,0:T(8,128)(2,1)S(1)} %pad_maximum_fusion.1), channel_id=1, source_target_pairs={{0,2},{1,3},{2,0},{3,1},{4,6},{5,7},{6,4},{7,5},{8,10},{9,11},{10,... | collective-permute-start | bytes 1572872 | tf_op jit(solution)/shard_map/ppermute | solution.py:110
  85.7 2.7 %collective-permute-start.3 = (bf16[128,4096]{1,0:T(8,128)(2,1)S(1)}, bf16[128,4096]{1,0:T(8,128)(2,1)S(1)}, u32[]{:S(2)}, u32[]{:S(2)}) collective-permute-start(bf16[128,4096]{1,0:T(8,128)(2,1)S(1)} %pad_maximum_fusion), channel_id=1, source_target_pairs={{0,1},{1,0},{2,3},{3,2},{4,5},{5,4},{6,7},{7,6},{8,9},{9,8},{10,11... | collective-permute-start | bytes 3145736 | tf_op jit(solution)/shard_map/ppermute | solution.py:110
